TPU v7x, 32 devices: a whole 2x2x4 slice. The times are simulated.
32 devices in a mesh: chan: 2 (over x), vis: 2 (over core), pix: 8 (over z, y).
Axes of the slice: x: 2, y: 2, z: 4, core: 2. Of those that a mesh axis runs over, the one named last changes fastest.
Arguments:
- response: bfloat16 [16384, 49152], P(('chan', 'vis'), 'pix'), parts along dimension 0, may hold values from -5 to 5
- vis_data: float32 [16384], P(('chan', 'vis')), parts along dimension 0, may hold values from -6 to 6
- baseline_of_row: int32 [8192], P('vis'), may hold values from 0 to 8191
- noise_class: int32 [8192], P('vis'), may hold values from 0 to 15
- baseline_weight: float32 [8192], replicated, may hold values from 0.25 to 4
- class_inv_var: float32 [32], P('chan'), parts along dimension 0, may hold values from 0.25 to 4
Outputs:
- sky_map: float32 [98304], P(('chan', 'pix')), parts along dimension 0
- psf: float32 [98304, 64], P(('chan', 'pix'), 'vis'), parts along dimension 0
There are 2 independent parts, one for each index of `chan`. A program takes and returns all parts, laid end to end along the dimension named above; an argument that names none is the same for every part. Nothing has to cross between parts.
Inputs may be any that keep to these rules, and one draw needn't show every extreme that they name: `baseline_of_row`: baseline index of each row.
All inputs are finite; a program needn't handle non-finite values.
Results may differ from a plain program's by a relative error of at most 0.0041.
Values may be sent and summed in bfloat16 or wider, within the bound.
No kernel may reach another device: no remote copies, remote signals or barrier semaphores. Data moves between devices by JAX's collectives and lax.ppermute only.
A program may use at most 128 MiB of HBM per device.

v0:
```python
import jax
import jax.numpy as jnp
from jax import lax
from jax.sharding import PartitionSpec as P

PANEL_DEV = 8


def shards(response, vis_data, baseline_of_row, noise_class, baseline_weight, class_inv_var):
    classes = lax.broadcasted_iota(jnp.int32, (1, class_inv_var.shape[0]), 1)
    class_weight = jnp.sum(
        jnp.where(noise_class[:, None] == classes, class_inv_var[None, :], jnp.float32(0.0)), axis=1
    )
    weight_row = jnp.take(baseline_weight, baseline_of_row) * class_weight
    own_panel = response[:, :PANEL_DEV]
    pix_rows = response.shape[1]
    piece_cols = lax.all_gather(own_panel, "pix", axis=1, tiled=True)
    operand = (weight_row[:, None] * piece_cols.astype(jnp.float32)).astype(jnp.bfloat16)
    plain_f = piece_cols.astype(jnp.float32)
    beam_part = jnp.concatenate(
        [
            lax.dot_general(
                response, operand, (((0,), (0,)), ((), ())), preferred_element_type=jnp.float32
            ),
            jnp.sum(weight_row[:, None] * plain_f * plain_f, axis=0)[None, :],
        ],
        axis=0,
    )
    weighted_vis = (weight_row * vis_data).astype(jnp.bfloat16)
    dirty_part = jnp.dot(weighted_vis, response, preferred_element_type=jnp.float32)
    norm_part = jnp.sum(weight_row[:, None] * jnp.square(response.astype(jnp.float32)), axis=0)
    col_share = beam_part.shape[1] // lax.axis_size("vis")
    beam_all, dirty_map, pixel_norm = lax.psum((beam_part, dirty_part, norm_part), "vis")
    beam_rows = lax.dynamic_slice_in_dim(beam_all, lax.axis_index("vis") * col_share, col_share, 1)
    panel_scale = beam_rows[pix_rows]
    beam_rows = beam_rows[:pix_rows]
    sky_map = dirty_map / jnp.sqrt(pixel_norm)
    psf = beam_rows / jnp.sqrt(pixel_norm[:, None] * panel_scale[None, :])
    return (sky_map, psf)


def solution(mesh):
    placed = (P(("chan", "vis"), "pix"), P(("chan", "vis")), P("vis"), P("vis"), P(), P("chan"))
    return jax.shard_map(
        shards,
        mesh=mesh,
        in_specs=placed,
        out_specs=(P(("chan", "pix")), P(("chan", "pix"), "vis")),
        check_vma=False,
    )
```

profile of v0, /device:TPU:0, one launch (start us, length us, event | category | flops | bytes accessed | tf_op | source)
XLA Modules:
  0.0 140.9 jit_solution(5494770655249392284)
XLA Ops:
  7.2 0.0 copy-start
  7.2 0.0 all-reduce.3.cloned.1.call-start
  7.2 0.7 fusion.2
  8.0 1.3 slice.9
  9.2 0.3 copy.14
  9.6 33.0 %all_gather.3 = bf16[4096,64]{0,1:T(8,128)(2,1)S(1)} all-gather(bf16[4096,8]{0,1:T(8,128)(2,1)S(1)} %copy.14), channel_id=1, replica_groups=mesh['chan'=2,'vis'=2,'pix'=8] {'pix'}, dimensions={1}, use_global_device_ids=true | all-gather | bytes 589824 | tf_op jit(solution)/shard_map/all_gather | solution.py:17
  42.6 0.0 copy-done
  42.6 23.0 %gather_fusion = f32[4096]{0:T(1024)S(1)} fusion(f32[8192]{0:T(1024)S(1)} %copy-done, s32[4096]{0:T(1024)S(1)} %fusion.2), kind=kCustom, calls=%fused_computation | custom fusion | bytes 49152 | tf_op jit(solution)/shard_map/jit(_take)/gather | solution.py:14
  65.6 0.9 select_reduce_fusion
  66.5 0.8 multiply_convert_fusion.2
  67.2 19.8 %convolution_bitcast_fusion = f32[6144,64]{0,1:T(8,128)S(1)} fusion(bf16[4096,6144]{1,0:T(8,128)(2,1)} %param.6, bf16[4096,64]{0,1:T(8,128)(2,1)S(1)} %all_gather.3, f32[4096]{0:T(1024)S(1)} %get-tuple-element.5), kind=kOutput, calls=%fused_computation.2 | convolution fusion | flops 3222011904 | bytes 52445184 | tf_op jit(solution)/shard_map/dot_general | solution.py:22
  87.1 0.2 fusion
  87.3 0.1 copy.13
  87.4 1.3 pad_maximum_fusion
  88.7 0.0 all-reduce.3.cloned.1.call-update
  88.7 19.3 %multiply_reduce_fusion = f32[6144]{0:T(1024)S(1)} fusion(bf16[4096,6144]{1,0:T(8,128)(2,1)} %param.6, f32[4096]{0:T(1024)S(1)} %get-tuple-element.5), kind=kLoop, calls=%fused_computation.1 | loop fusion | flops 100657152 | bytes 50372608 | tf_op jit(solution)/shard_map/reduce_sum | solution.py:31
  108.0 18.9 %fusion.3 = f32[1,6144]{1,0:T(1,128)S(1)} fusion(bf16[4096,1]{0,1:T(2,128)(2,1)S(1)} %reshape.26, bf16[4096,6144]{1,0:T(8,128)(2,1)} %param.6), kind=kOutput, calls=%fused_computation.17 | convolution fusion | flops 50331648 | bytes 50364416 | tf_op jit(solution)/shard_map/dot_general | solution.py:30
  126.9 3.5 %all-reduce = (f32[6144]{0:T(1024)S(1)}, f32[6144]{0:T(1024)S(1)}) all-reduce(f32[6144]{0:T(1024)S(1)} %bitcast.7, f32[6144]{0:T(1024)S(1)} %multiply_reduce_fusion), channel_id=1, replica_groups=mesh['chan'=2,'vis'=2,'pix'=8] {'vis'}, use_global_device_ids=true, to_apply=%region_1.2 | all-reduce | flops 12288 | bytes 98304 | tf_op jit(solution)/shard_map/psum | solution.py:33
  130.4 0.6 rsqrt_multiply_fusion
  131.1 0.0 all-reduce.3.cloned.1.call-done
  131.1 0.8 dynamic-slice_reduce_fusion
  131.9 2.2 %dynamic-slice_multiply_fusion = f32[6144,32]{0,1:T(8,128)} fusion(f32[6145,64]{0,1:T(8,128)} %all-reduce.3.cloned.1.call-done, s32[]{:T(128)S(6)} %select_n.21, f32[32]{0:T(128)S(1)} %dynamic-slice_reduce_fusion, f32[6144]{0:T(1024)S(1)} %get-tuple-element.3), kind=kLoop, calls=%fused_computation.7 | loop fusion | flops 393216 | bytes 1597572 | tf_op jit(solution)/shard_map/div | solution.py:38
  (1 shorter events, 0.0 us)
Async XLA Ops:
  7.2 35.4 %copy-start = (f32[8192]{0:T(1024)S(1)}, f32[8192]{0:T(1024)}, u32[]{:S(2)}) copy-start(f32[8192]{0:T(1024)} %param.10) | copy-start | bytes 98308
  7.2 123.9 %all-reduce.3.cloned.1.call-start = ((), (), s32[]{:S(2)}) async-start(), calls=%async_computation | async-start | bytes 3211264 | tf_op jit(solution)/shard_map/psum | solution.py:33
Sparse Core Ops, SparseCore 0:
  88.8 21.5 all-reduce.2
where the time goes:
time: 142 us; the launch traced here: 141 us
  matrix products  38.7 us (27%)
  blocking collectives  36.6 us (26%)
  other arithmetic  26 us (18%)
  local copies, waits for them, and re-layouts  25.6 us (18%)
  between operations  14.1 us (10%)
    all_gather x1, blocking collectives, shards(): piece_cols = lax.all_gather(own_panel, 'pix', axis=1, tiled=True)  33 us
    gather x1, local copies, waits for them, and re-layouts, shards(): weight_row = jnp.take(baseline_weight, baseline_of_row) * class_weight  23 us
    dot_general x1, matrix products, shards(): lax.dot_general(response, operand, (((0,), (0,)), ((), ())), preferred_el...  19.8 us
    reduce_sum x1, other arithmetic, shards(): jnp.sum(weight_row[:, None] * jnp.square(response.astype(jnp.float32)), a...  19.3 us
    dot_general x1, matrix products, shards(): jnp.dot(weighted_vis, response, preferred_element_type=jnp.float32)  18.9 us
    psum x1, blocking collectives, shards(): lax.psum((beam_part, dirty_part, norm_part), 'vis')  3.53 us
  transfers between devices with their start and end apart: 1, of which 0 were waited for; matrix products, arithmetic and copies ran while one was open for 28% of the time, Pallas kernels for 0%

commit v1 on v0

--- a/solution.py
+++ b/solution.py
@@ -14,7 +14,9 @@
     weight_row = jnp.take(baseline_weight, baseline_of_row) * class_weight
     own_panel = response[:, :PANEL_DEV]
     pix_rows = response.shape[1]
-    piece_cols = lax.all_gather(own_panel, "pix", axis=1, tiled=True)
+    piece_cols = jnp.concatenate(
+        lax.all_to_all(jnp.stack([own_panel] * lax.axis_size("pix")), "pix", 0, 0), axis=1
+    )
     operand = (weight_row[:, None] * piece_cols.astype(jnp.float32)).astype(jnp.bfloat16)
     plain_f = piece_cols.astype(jnp.float32)
     beam_part = jnp.concatenate(

time: 142 us -> 117 us (0.82)
  blocking collectives: 36.6 us -> 3.53 us
  starting transfers between devices: 0.04 us -> 7.35 us
    all_gather x1 -> x0, blocking collectives: 33 us -> none  [shards(): piece_cols = lax.all_gather(own_panel, 'pix', axis=1, tiled=True)]
    all_to_all x0 -> x1, starting transfers between devices: none -> 7.31 us  [shards(): lax.all_to_all(jnp.stack([own_panel] * lax.axis_size('pix')), 'pix', 0, 0)]
  transfers between devices with their start and end apart: 1 -> 2, of which waited for: 0 -> 0; matrix products, arithmetic and copies ran while one was open for 28% -> 56% of each run, Pallas kernels for 0% -> 0%
where the time goes in v1:
time: 117 us
  matrix products  39.3 us (34%)
  local copies, waits for them, and re-layouts  26.4 us (23%)
  other arithmetic  25.9 us (22%)
  between operations  14.1 us (12%)
  starting transfers between devices  7.35 us (6%)
  blocking collectives  3.53 us (3%)
    gather x1, local copies, waits for them, and re-layouts, shards(): weight_row = jnp.take(baseline_weight, baseline_of_row) * class_weight  23 us
    dot_general x1, matrix products, shards(): lax.dot_general(response, operand, (((0,), (0,)), ((), ())), preferred_el...  19.8 us
    dot_general x1, matrix products, shards(): jnp.dot(weighted_vis, response, preferred_element_type=jnp.float32)  19.5 us
    reduce_sum x1, other arithmetic, shards(): jnp.sum(weight_row[:, None] * jnp.square(response.astype(jnp.float32)), a...  19.3 us
    all_to_all x1, starting transfers between devices, shards(): lax.all_to_all(jnp.stack([own_panel] * lax.axis_size('pix')), 'pix', 0, 0)  7.31 us
    psum x1, blocking collectives, shards(): lax.psum((beam_part, dirty_part, norm_part), 'vis')  3.53 us
  transfers between devices with their start and end apart: 2, of which 0 were waited for; matrix products, arithmetic and copies ran while one was open for 56% of the time, Pallas kernels for 0%

profile of v1, /device:TPU:0, one launch (start us, length us, event | category | flops | bytes accessed | tf_op | source)
XLA Modules:
  0.0 116.6 jit_solution(17258936268169019747)
XLA Ops:
  7.2 0.0 copy-start
  7.2 1.3 %slice.9 = bf16[4096,8]{1,0:T(8,128)(2,1)S(1)} slice(bf16[4096,6144]{1,0:T(8,128)(2,1)} %param.6), slice={[0:4096], [0:8]} | slice | bytes 131072 | tf_op jit(solution)/shard_map/slice | solution.py:15
  8.5 0.3 copy.11
  8.8 0.8 stack.2
  9.6 7.3 %all-to-all-start = ((bf16[8,4096,8]{1,2,0:T(8,128)(2,1)}), bf16[8,4096,8]{1,2,0:T(8,128)(2,1)S(1)}, u32[]{:S(2)}, u32[]{:S(2)}) async-start(bf16[8,4096,8]{1,2,0:T(8,128)(2,1)} %stack.2), calls=%async_computation | async-start | bytes 1048576 | tf_op jit(solution)/shard_map/all_to_all | solution.py:18
  16.9 0.0 all-reduce.3.cloned.1.call-start
  17.0 0.7 fusion.5
  17.7 0.0 copy-done
  17.7 23.0 %gather_fusion = f32[4096]{0:T(1024)S(1)} fusion(f32[8192]{0:T(1024)S(1)} %copy-done, s32[4096]{0:T(1024)S(1)} %fusion.5), kind=kCustom, calls=%fused_computation | custom fusion | bytes 49152 | tf_op jit(solution)/shard_map/jit(_take)/gather | solution.py:14
  40.7 0.9 select_reduce_fusion
  41.6 0.8 multiply_convert_fusion
  42.4 19.3 %multiply_reduce_fusion = f32[6144]{0:T(1024)S(1)} fusion(bf16[4096,6144]{1,0:T(8,128)(2,1)} %param.6, f32[4096]{0:T(1024)S(1)} %get-tuple-element.5), kind=kLoop, calls=%fused_computation.1 | loop fusion | flops 100657152 | bytes 50372608 | tf_op jit(solution)/shard_map/reduce_sum | solution.py:33
  61.7 0.0 all-to-all-done
  61.7 0.2 fusion.2
  61.9 0.1 broadcast_in_dim.34
  62.0 19.8 %convolution_bitcast_fusion = f32[6144,64]{0,1:T(8,128)S(1)} fusion(bf16[4096,6144]{1,0:T(8,128)(2,1)} %param.6, bf16[8,4096,8]{1,2,0:T(8,128)(2,1)S(1)} %all-to-all-done, f32[4096]{0:T(1024)S(1)} %get-tuple-element.5), kind=kOutput, calls=%fused_computation.2 | convolution fusion | flops 3222011904 | bytes 52445184 | tf_op jit(solution)/shard_map/dot_general | solution.py:24
  81.8 1.3 %pad_maximum_fusion = f32[6145,64]{0,1:T(8,128)} fusion(f32[1,64]{0,1:T(8,128)S(1)} %broadcast_in_dim.34, f32[6144,64]{0,1:T(8,128)S(1)} %convolution_bitcast_fusion), kind=kLoop, calls=%fused_computation.3 | loop fusion | flops 393280 | bytes 3146240 | tf_op jit(solution)/shard_map/concatenate | solution.py:22
  83.1 0.0 all-reduce.3.cloned.1.call-update
  83.1 19.5 %fusion.6 = f32[1,6144]{1,0:T(1,128)S(1)} fusion(bf16[4096,1]{0,1:T(2,128)(2,1)S(1)} %reshape.40, bf16[4096,6144]{1,0:T(8,128)(2,1)} %param.6), kind=kOutput, calls=%fused_computation.20 | convolution fusion | flops 50331648 | bytes 50364416 | tf_op jit(solution)/shard_map/dot_general | solution.py:32
  102.6 3.5 %all-reduce = (f32[6144]{0:T(1024)S(1)}, f32[6144]{0:T(1024)S(1)}) all-reduce(f32[6144]{0:T(1024)S(1)} %bitcast.20, f32[6144]{0:T(1024)S(1)} %multiply_reduce_fusion), channel_id=1, replica_groups=mesh['chan'=2,'vis'=2,'pix'=8] {'vis'}, use_global_device_ids=true, to_apply=%region_1.2 | all-reduce | flops 12288 | bytes 98304 | tf_op jit(solution)/shard_map/psum | solution.py:35
  106.1 0.6 rsqrt_multiply_fusion
  106.8 0.0 all-reduce.3.cloned.1.call-done
  106.8 0.8 dynamic-slice_reduce_fusion
  107.6 2.2 %dynamic-slice_multiply_fusion = f32[6144,32]{0,1:T(8,128)} fusion(f32[6145,64]{0,1:T(8,128)} %all-reduce.3.cloned.1.call-done, s32[]{:T(128)S(6)} %select_n.21, f32[32]{0:T(128)S(1)} %dynamic-slice_reduce_fusion, f32[6144]{0:T(1024)S(1)} %get-tuple-element.3), kind=kLoop, calls=%fused_computation.10 | loop fusion | flops 393216 | bytes 1597572 | tf_op jit(solution)/shard_map/div | solution.py:40
  (1 shorter events, 0.0 us)
Async XLA Ops:
  7.2 10.5 %copy-start = (f32[8192]{0:T(1024)S(1)}, f32[8192]{0:T(1024)}, u32[]{:S(2)}) copy-start(f32[8192]{0:T(1024)} %param.10) | copy-start | bytes 98308
  9.6 52.0 %all-to-all-start = ((bf16[8,4096,8]{1,2,0:T(8,128)(2,1)}), bf16[8,4096,8]{1,2,0:T(8,128)(2,1)S(1)}, u32[]{:S(2)}, u32[]{:S(2)}) async-start(bf16[8,4096,8]{1,2,0:T(8,128)(2,1)} %stack.2), calls=%async_computation | async-start | bytes 1048576 | tf_op jit(solution)/shard_map/all_to_all | solution.py:18
  16.9 89.8 %all-reduce.3.cloned.1.call-start = ((), (), s32[]{:S(2)}) async-start(), calls=%async_computation.1 | async-start | bytes 3211264 | tf_op jit(solution)/shard_map/psum | solution.py:35
Sparse Core Ops, SparseCore 0:
  83.2 21.7 all-reduce.2
